TPU v7x, 32 devices: a whole 2x2x4 slice. The times are simulated.
32 devices in a mesh: tm: 8 (over y, x, core), tx: 4 (over z).
Axes of the slice: x: 2, y: 2, z: 4, core: 2. Of those that a mesh axis runs over, the one named last changes fastest.
Arguments:
- state: float32 [8, 64, 256, 128], P('tm', 'tx'), may hold values from -6 to 6
- force: float32 [8, 64, 256, 128], P('tm', 'tx'), may hold values from -6 to 6
- u_init: float32 [64, 256, 128], P('tx'), may hold values from -6 to 6
- kappa: float32 [64, 256], P('tx'), may hold values from 0.1 to 2
- rates: float32 [128], replicated, may hold values from 0.05 to 4
- basis: float32 [128, 128], replicated, may hold values from -1 to 1, as said below
Outputs:
- correction: float32 [8, 64, 256, 128], P('tm', 'tx')
Inputs may be any that keep to these rules, and one draw needn't show every extreme that they name: basis is an orthogonal matrix.
All inputs are finite; a program needn't handle non-finite values.
Results may differ from a plain program's by a relative error of at most 0.0003.
Values sent between devices are 32-bit elements; how exact they have to be, the bound alone decides.
No kernel may reach another device: no remote copies, remote signals or barrier semaphores. Data moves between devices by JAX's collectives and lax.ppermute only.
A program may use at most 64 MiB of HBM per device.

v0:
```python
import math
import jax
import jax.numpy as jnp
from jax import lax
from jax.sharding import PartitionSpec as P

ALPHA = 0.05
TWO_PI = 2.0 * math.pi


def extended(block, sides, width):
    for axis, dim in sides:
        count = lax.axis_size(axis)
        forward = [(i, i + 1) for i in range(count - 1)]
        backward = [(target, source) for source, target in forward]
        low = lax.ppermute(
            lax.slice_in_dim(block, block.shape[dim] - width, None, axis=dim), axis, forward
        )
        high = lax.ppermute(lax.slice_in_dim(block, 0, width, axis=dim), axis, backward)
        block = jnp.concatenate([low, block, high], axis=dim)
    return block


def from_behind(array, axis, by):
    count = lax.axis_size(axis)
    pairs = [(i, i + by) for i in range(count) if 0 <= i + by < count]
    return lax.ppermute(array, axis, pairs)


def neighbours(padded):
    return (
        padded[..., 2:, 1:-1, :]
        + padded[..., :-2, 1:-1, :]
        + padded[..., 1:-1, 2:, :]
        + padded[..., 1:-1, :-2, :]
    )


def relax(source, kappa_b, real_den, imag_den, rims):
    magnitude = real_den * real_den + imag_den * imag_den

    def divide(numer):
        return jnp.stack(
            [
                (numer[0] * real_den + numer[1] * imag_den) / magnitude,
                (numer[1] * real_den - numer[0] * imag_den) / magnitude,
            ]
        )

    field = divide(source)
    for repeat in range(2):
        field = divide(source + kappa_b * rims(field))
    return field


def cell_rims(field):
    padded = extended(field, (("tm", 3), ("tx", 2)), 1)
    return neighbours(padded)


def on_device(state, force, u_init, kappa, rates, basis):
    highest = lax.Precision.HIGHEST
    column_size = state.shape[3]
    steps_total = lax.axis_size("tm")
    here = lax.axis_index("tm")
    earlier = from_behind(state, "tm", 1)
    earlier = jnp.where(here == 0, u_init[None], earlier)
    padded = extended(state, (("tx", 1),), 1)
    padded = jnp.pad(padded, ((0, 0), (0, 0), (1, 1), (0, 0)))
    beside_all = neighbours(padded)
    coords = jnp.dot(state.reshape(-1, column_size), basis, precision=highest)
    vertical = jnp.dot(coords * rates, basis.T, precision=highest).reshape(state.shape)
    kappa_b = kappa[None, :, :, None]
    residual = (
        force
        - (state - earlier)
        - vertical
        - kappa_b * (4.0 * state - beside_all)
        - 0.5 * state**3 / (1.0 + state * state)
    )
    modal = jnp.dot(residual.reshape(-1, column_size), basis, precision=highest).reshape(
        state.shape
    )
    decay = jnp.log(ALPHA) / steps_total
    scaled = modal * jnp.exp(decay * here.astype(jnp.float32))
    gathered = lax.all_to_all(scaled, "tm", split_axis=2, concat_axis=0, tiled=True)
    block_y = gathered.shape[2]
    indices = jnp.arange(steps_total)
    steps_f = indices.astype(jnp.float32)
    products = (indices[:, None] * indices[None, :] % steps_total).astype(jnp.float32)
    angles = TWO_PI * products / steps_total
    cosine = jnp.cos(angles)
    sine = jnp.sin(angles)
    flat_cells = gathered.reshape(steps_total, -1)
    spectrum = jnp.stack(
        [
            jnp.dot(cosine, flat_cells, precision=highest),
            -jnp.dot(sine, flat_cells, precision=highest),
        ]
    ).reshape((2,) + gathered.shape)
    factor = jnp.exp(decay)
    theta = TWO_PI * steps_f / steps_total
    shift_re = 1.0 - factor * jnp.cos(theta)
    shift_im = factor * jnp.sin(theta)
    start = here * block_y
    kappa_cells = lax.dynamic_slice_in_dim(kappa, start, block_y, 1)[None, :, :, None]
    real_den = shift_re[:, None, None, None] + rates + 4.0 * kappa_cells
    imag_den = shift_im[:, None, None, None] + jnp.zeros_like(real_den)
    solved = relax(spectrum, kappa_cells, real_den, imag_den, cell_rims)
    flat_re = solved[0].reshape(steps_total, -1)
    flat_im = solved[1].reshape(steps_total, -1)
    times = (
        jnp.dot(cosine, flat_re, precision=highest) - jnp.dot(sine, flat_im, precision=highest)
    ) / steps_total
    times = times * jnp.exp(-decay * steps_f)[:, None]
    back = lax.all_to_all(
        times.reshape(gathered.shape), "tm", split_axis=0, concat_axis=2, tiled=True
    )
    return jnp.dot(back.reshape(-1, column_size), basis.T, precision=highest).reshape(state.shape)


def solution(mesh):
    return jax.shard_map(
        on_device,
        mesh=mesh,
        in_specs=(
            P("tm", "tx", None, None),
            P("tm", "tx", None, None),
            P("tx", None, None),
            P("tx", None),
            P(),
            P(),
        ),
        out_specs=P("tm", "tx", None, None),
        check_vma=False,
    )
```

profile of v0, /device:TPU:0, one launch (start us, length us, event | category | flops | bytes accessed | tf_op | source)
XLA Modules:
  0.0 164.9 jit_solution(18260656128730488843)
XLA Ops:
  0.0 3.9 %collective-permute-start = (f32[1,16,256,128]{3,2,1,0:T(8,128)}, f32[1,16,256,128]{3,2,1,0:T(8,128)}, u32[]{:S(2)}, u32[]{:S(2)}) collective-permute-start(f32[1,16,256,128]{3,2,1,0:T(8,128)} %param.6), channel_id=1, source_target_pairs={{0,4},{4,8},{8,12},{12,16},{16,20},{20,24},{24,28},{1,5},{5,9},{9,... | collective-permute-start | bytes 6291464 | tf_op jit(solution)/shard_map/ppermute | solution.py:27
  6.2 4.9 %collective-permute-start.2 = (f32[1,1,256,128]{3,2,1,0:T(8,128)S(1)}, f32[1,1,256,128]{3,2,1,0:T(8,128)S(1)}, u32[]{:S(2)}, u32[]{:S(2)}) collective-permute-start(f32[1,1,256,128]{3,2,1,0:T(8,128)S(1)} %get-tuple-element.21), channel_id=1, source_target_pairs={{0,1},{1,2},{2,3},{4,5},{5,6},{6,7},{8,9},{9,10},{10,11},{12,13},{... | collective-permute-start | bytes 393224 | tf_op jit(solution)/shard_map/ppermute | solution.py:16
  11.1 3.4 %convolution_multiply_fusion = f32[4096,128]{1,0:T(8,128)S(1)} fusion(f32[4096,128]{1,0:T(8,128)} %bitcast.61, f32[128,128]{1,0:T(8,128)S(1)} %copy-done, f32[128]{0:T(128)} %param.10), kind=kOutput, calls=%fused_computation.8 | convolution fusion | flops 805830656 | bytes 4260352 | tf_op jit(solution)/shard_map/dot_general | solution.py:71
  14.6 3.1 %fusion.96 = f32[4096,128]{1,0:T(8,128)} fusion(f32[4096,128]{1,0:T(8,128)S(1)} %convolution_multiply_fusion, f32[128,128]{1,0:T(8,128)S(1)} %copy-done), kind=kOutput, calls=%fused_computation.159 | convolution fusion | flops 805306368 | bytes 4259840 | tf_op jit(solution)/shard_map/dot_general | solution.py:72
  20.0 4.9 %multiply_bitcast_fusion = f32[1,16,256,128]{3,2,1,0:T(8,128)S(1)} fusion(f32[1,16,256,128]{3,2,1,0:T(8,128)S(1)} %copy-done.1, f32[1,18,258,128]{3,2,1,0:T(8,128)S(1)} %select_maximum_fusion, f32[1,1,256,128]{3,2,1,0:T(8,128)S(1)} %collective-permute-done.2, f32[1,1,256,128]{3,2,1,0:T(8,128)S(1)} %collective-permute-done.1, ...), kind=kOutput, calls=%fused_computation.87 | convolution fusion | flops 815792128 | bytes 17121284 | tf_op jit(solution)/shard_map/dot_general | solution.py:81
  24.9 2.5 %copy.10 = f32[1,16,256,128]{3,1,0,2:T(8,128)} copy(f32[1,16,256,128]{3,2,1,0:T(8,128)S(1)} %multiply_bitcast_fusion) | data formatting | bytes 4194304 | tf_op jit(solution)/shard_map/mul | solution.py:85
  27.4 13.5 %all-to-all-start = ((f32[1,16,256,128]{3,1,0,2:T(8,128)}), f32[1,16,256,128]{3,1,0,2:T(8,128)S(1)}, u32[]{:S(2)}, u32[]{:S(2)}) async-start(f32[1,16,256,128]{3,1,0,2:T(8,128)} %copy.10), calls=%async_computation | async-start | bytes 4194304 | tf_op jit(solution)/shard_map/all_to_all | solution.py:86
  41.2 26.4 %all-to-all-done = f32[1,16,256,128]{3,1,0,2:T(8,128)S(1)} async-done(((f32[1,16,256,128]{3,1,0,2:T(8,128)}), f32[1,16,256,128]{3,1,0,2:T(8,128)S(1)}, u32[]{:S(2)}, u32[]{:S(2)}) %all-to-all-start) | async-done | bytes 2097184 | tf_op jit(solution)/shard_map/all_to_all | solution.py:86
  67.6 1.9 %copy.15 = f32[1,16,8,32,128]{4,3,1,2,0:T(8,128)} copy(f32[1,16,8,32,128]{4,1,3,2,0:T(8,128)S(1)} %bitcast.62) | data formatting | bytes 4194304 | tf_op jit(solution)/shard_map/all_to_all | solution.py:86
  69.5 2.0 %reshape.165 = f32[8,65536]{1,0:T(8,128)S(1)} reshape(f32[8,1,16,32,128]{4,3,2,0,1:T(8,128)} %bitcast.63) | data formatting | bytes 4194304 | tf_op jit(solution)/shard_map/reshape | solution.py:94
  79.0 2.7 %collective-permute-done.4 = f32[2,8,16,1,128]{4,1,3,2,0:T(8,128)S(1)} collective-permute-done((f32[2,8,16,1,128]{4,1,3,2,0:T(8,128)S(1)}, f32[2,8,16,1,128]{4,1,3,2,0:T(8,128)S(1)}, u32[]{:S(2)}, u32[]{:S(2)}) %collective-permute-start.4) | collective-permute-done | bytes 131104 | tf_op jit(solution)/shard_map/ppermute | solution.py:19
  83.0 4.6 %collective-permute-start.6 = (f32[2,8,1,34,128]{4,1,3,2,0:T(8,128)S(1)}, f32[2,8,1,34,128]{4,1,3,2,0:T(8,128)S(1)}, u32[]{:S(2)}, u32[]{:S(2)}) collective-permute-start(f32[2,8,1,34,128]{4,1,3,2,0:T(8,128)S(1)} %get-tuple-element.10), channel_id=1, source_target_pairs={{0,1},{1,2},{2,3},{4,5},{5,6},{6,7},{8,9},{9,10},{10,11},{12,13},{... | collective-permute-start | bytes 835592 | tf_op jit(solution)/shard_map/ppermute | solution.py:16
  87.6 3.0 %collective-permute-done.5 = f32[2,8,1,34,128]{4,1,3,2,0:T(8,128)S(1)} collective-permute-done((f32[2,8,1,34,128]{4,1,3,2,0:T(8,128)S(1)}, f32[2,8,1,34,128]{4,1,3,2,0:T(8,128)S(1)}, u32[]{:S(2)}, u32[]{:S(2)}) %collective-permute-start.5) | collective-permute-done | bytes 278560 | tf_op jit(solution)/shard_map/ppermute | solution.py:19
  92.3 3.6 %fusion.8 = f32[2,8,16,32,128]{4,1,3,2,0:T(8,128)S(1)} fusion(f32[2,8,16,1,128]{4,1,3,2,0:T(8,128)S(1)} %collective-permute-done.3, f32[1,8,16,32,128]{4,1,3,2,0:T(8,128)S(1)} %get-tuple-element.14, f32[1,8,16,32,128]{4,1,3,2,0:T(8,128)S(1)} %get-tuple-element.13, f32[2,8,16,1,128]{4,1,3,2,0:T(8,128)S(1)} %collective-permute-done.4, ...), kind=kLoop, calls=%fused_computation.29 | loop fusion | flops 18874368 | bytes 13404160 | tf_op jit(solution)/shard_map/add | solution.py:52
  97.0 4.3 %collective-permute-start.7 = (f32[2,8,16,1,128]{4,1,3,2,0:T(8,128)S(1)}, f32[2,8,16,1,128]{4,1,3,2,0:T(8,128)S(1)}, u32[]{:S(2)}, u32[]{:S(2)}) collective-permute-start(f32[2,8,16,1,128]{4,1,3,2,0:T(8,128)S(1)} %get-tuple-element.18), channel_id=1, source_target_pairs={{0,4},{4,8},{8,12},{12,16},{16,20},{20,24},{24,28},{1,5},{5,9},{9,... | collective-permute-start | bytes 393224 | tf_op jit(solution)/shard_map/ppermute | solution.py:16
  102.7 3.3 %collective-permute-done.8 = f32[2,8,16,1,128]{4,1,3,2,0:T(8,128)S(1)} collective-permute-done((f32[2,8,16,1,128]{4,1,3,2,0:T(8,128)S(1)}, f32[2,8,16,1,128]{4,1,3,2,0:T(8,128)S(1)}, u32[]{:S(2)}, u32[]{:S(2)}) %collective-permute-start.8) | collective-permute-done | bytes 131104 | tf_op jit(solution)/shard_map/ppermute | solution.py:19
  106.0 4.4 %collective-permute-start.10 = (f32[2,8,1,34,128]{4,1,3,2,0:T(8,128)S(1)}, f32[2,8,1,34,128]{4,1,3,2,0:T(8,128)S(1)}, u32[]{:S(2)}, u32[]{:S(2)}) collective-permute-start(f32[2,8,1,34,128]{4,1,3,2,0:T(8,128)S(1)} %get-tuple-element.8), channel_id=1, source_target_pairs={{0,1},{1,2},{2,3},{4,5},{5,6},{6,7},{8,9},{9,10},{10,11},{12,13},{... | collective-permute-start | bytes 835592 | tf_op jit(solution)/shard_map/ppermute | solution.py:16
  112.0 2.9 %collective-permute-done.10 = f32[2,8,1,34,128]{4,1,3,2,0:T(8,128)S(1)} collective-permute-done((f32[2,8,1,34,128]{4,1,3,2,0:T(8,128)S(1)}, f32[2,8,1,34,128]{4,1,3,2,0:T(8,128)S(1)}, u32[]{:S(2)}, u32[]{:S(2)}) %collective-permute-start.10) | collective-permute-done | bytes 278560 | tf_op jit(solution)/shard_map/ppermute | solution.py:16
  114.9 4.7 %collective-permute-done.9 = f32[2,8,1,34,128]{4,1,3,2,0:T(8,128)S(1)} collective-permute-done((f32[2,8,1,34,128]{4,1,3,2,0:T(8,128)S(1)}, f32[2,8,1,34,128]{4,1,3,2,0:T(8,128)S(1)}, u32[]{:S(2)}, u32[]{:S(2)}) %collective-permute-start.9) | collective-permute-done | bytes 278560 | tf_op jit(solution)/shard_map/ppermute | solution.py:19
  119.6 3.6 %fusion.3 = f32[2,8,16,32,128]{4,1,3,2,0:T(8,128)S(1)} fusion(f32[2,8,16,1,128]{4,1,3,2,0:T(8,128)S(1)} %collective-permute-done.7, f32[1,8,16,32,128]{4,1,3,2,0:T(8,128)S(1)} %get-tuple-element.12, f32[1,8,16,32,128]{4,1,3,2,0:T(8,128)S(1)} %get-tuple-element.11, f32[2,8,16,1,128]{4,1,3,2,0:T(8,128)S(1)} %collective-permute-done.8, ...), kind=kLoop, calls=%fused_computation.12 | loop fusion | flops 18874368 | bytes 13404160 | tf_op jit(solution)/shard_map/add | solution.py:52
  123.8 2.2 %fusion.36 = f32[8,65536]{1,0:T(8,128)S(1)} fusion(f32[8,65536]{1,0:T(8,128)S(1)} %bitcast.72, f32[8,65536]{1,0:T(8,128)S(1)} %bitcast.70, f32[8,65536]{1,0:T(8,128)S(1)} %bitcast.67, f32[8]{0:T(128)S(1)} %get-tuple-element.24, f32[8]{0:T(128)S(1)} %get-tuple-element.23, f32[65536]{0:T(1024)S(1)} %bitcast.74), kind=kOutput, calls=%fused_computation.81 | convolution fusion | flops 54002560 | bytes 8650816 | tf_op jit(solution)/shard_map/dot_general | solution.py:113
  126.1 2.4 %fusion = f32[8,65536]{1,0:T(8,128)S(1)} fusion(f32[8,65536]{1,0:T(8,128)S(1)} %fusion.36, f32[8,65536]{1,0:T(8,128)S(1)} %bitcast.71, f32[8,65536]{1,0:T(8,128)S(1)} %bitcast.73, f32[8,65536]{1,0:T(8,128)S(1)} %bitcast.68, f32[8]{0:T(128)S(1)} %exponential_multiply_fusion, f32[8]{0:T(128)S(1)} %get-tuple-element.24, f32[8]{0:T(128)S(1)} %get-tuple-element.23, ...), kind=kOutput, calls=%fused_computation.1 | convolution fusion | flops 55051136 | bytes 10748000 | tf_op jit(solution)/shard_map/dot_general | solution.py:113
  128.9 32.7 %all_to_all.30 = f32[8,16,32,128]{3,2,1,0:T(8,128)S(1)} all-to-all(f32[8,16,32,128]{3,2,1,0:T(8,128)S(1)} %copy.12), channel_id=1, replica_groups=mesh['tm'=8,'tx'=4] {'tm'}, dimensions={0} | all-to-all | bytes 4194304 | tf_op jit(solution)/shard_map/all_to_all | solution.py:116
  161.8 3.1 %convolution_bitcast_fusion = f32[1,16,256,128]{3,2,1,0:T(8,128)} fusion(f32[16,256,128]{2,1,0:T(8,128)S(1)} %bitcast.65, f32[128,128]{1,0:T(8,128)S(1)} %copy-done), kind=kOutput, calls=%fused_computation.91 | convolution fusion | flops 805306368 | bytes 4259840 | tf_op jit(solution)/shard_map/dot_general | solution.py:119
  (44 shorter events, 20.4 us)
Async XLA Ops:
  0.0 11.1 %copy-start = (f32[128,128]{1,0:T(8,128)S(1)}, f32[128,128]{1,0:T(8,128)}, u32[]{:S(2)}) copy-start(f32[128,128]{1,0:T(8,128)} %param.11) | copy-start | bytes 196612
  0.0 18.0 %collective-permute-start = (f32[1,16,256,128]{3,2,1,0:T(8,128)}, f32[1,16,256,128]{3,2,1,0:T(8,128)}, u32[]{:S(2)}, u32[]{:S(2)}) collective-permute-start(f32[1,16,256,128]{3,2,1,0:T(8,128)} %param.6), channel_id=1, source_target_pairs={{0,4},{4,8},{8,12},{12,16},{16,20},{20,24},{24,28},{1,5},{5,9},{9,... | collective-permute-start | bytes 6291464 | tf_op jit(solution)/shard_map/ppermute | solution.py:27
  4.9 12.9 %collective-permute-start.1 = (f32[1,1,256,128]{3,2,1,0:T(8,128)S(1)}, f32[1,1,256,128]{3,2,1,0:T(8,128)S(1)}, u32[]{:S(2)}, u32[]{:S(2)}) collective-permute-start(f32[1,1,256,128]{3,2,1,0:T(8,128)S(1)} %get-tuple-element.22), channel_id=1, source_target_pairs={{1,0},{2,1},{3,2},{5,4},{6,5},{7,6},{9,8},{10,9},{11,10},{13,12},{... | collective-permute-start | bytes 393224 | tf_op jit(solution)/shard_map/ppermute | solution.py:19
  6.2 11.6 %collective-permute-start.2 = (f32[1,1,256,128]{3,2,1,0:T(8,128)S(1)}, f32[1,1,256,128]{3,2,1,0:T(8,128)S(1)}, u32[]{:S(2)}, u32[]{:S(2)}) collective-permute-start(f32[1,1,256,128]{3,2,1,0:T(8,128)S(1)} %get-tuple-element.21), channel_id=1, source_target_pairs={{0,1},{1,2},{2,3},{4,5},{5,6},{6,7},{8,9},{9,10},{10,11},{12,13},{... | collective-permute-start | bytes 393224 | tf_op jit(solution)/shard_map/ppermute | solution.py:16
  14.6 3.2 %copy-start.1 = (f32[1,16,256,128]{3,2,1,0:T(8,128)S(1)}, f32[1,16,256,128]{3,2,1,0:T(8,128)}, u32[]{:S(2)}) copy-start(f32[1,16,256,128]{3,2,1,0:T(8,128)} %param.6) | copy-start | bytes 6291460
  17.7 1.6 copy-start.2
  17.7 1.6 copy-start.3
  17.8 2.2 %copy-start.5 = (f32[1,16,256,128]{3,2,1,0:T(8,128)S(1)}, f32[1,16,256,128]{3,2,1,0:T(8,128)}, u32[]{:S(2)}) copy-start(f32[1,16,256,128]{3,2,1,0:T(8,128)} %param.7) | copy-start | bytes 6291460
  27.4 13.7 %copy-start.4 = (f32[128]{0:T(128)S(1)}, f32[128]{0:T(128)}, u32[]{:S(2)}) copy-start(f32[128]{0:T(128)} %param.10) | copy-start | bytes 1540
  27.4 40.1 %all-to-all-start = ((f32[1,16,256,128]{3,1,0,2:T(8,128)}), f32[1,16,256,128]{3,1,0,2:T(8,128)S(1)}, u32[]{:S(2)}, u32[]{:S(2)}) async-start(f32[1,16,256,128]{3,1,0,2:T(8,128)} %copy.10), calls=%async_computation | async-start | bytes 4194304 | tf_op jit(solution)/shard_map/all_to_all | solution.py:86
  76.4 2.6 %collective-permute-start.3 = (f32[2,8,16,1,128]{4,1,3,2,0:T(8,128)S(1)}, f32[2,8,16,1,128]{4,1,3,2,0:T(8,128)S(1)}, u32[]{:S(2)}, u32[]{:S(2)}) collective-permute-start(f32[2,8,16,1,128]{4,1,3,2,0:T(8,128)S(1)} %get-tuple-element.20), channel_id=1, source_target_pairs={{0,4},{4,8},{8,12},{12,16},{16,20},{20,24},{24,28},{1,5},{5,9},{9,... | collective-permute-start | bytes 393224 | tf_op jit(solution)/shard_map/ppermute | solution.py:16
  77.7 4.0 %collective-permute-start.4 = (f32[2,8,16,1,128]{4,1,3,2,0:T(8,128)S(1)}, f32[2,8,16,1,128]{4,1,3,2,0:T(8,128)S(1)}, u32[]{:S(2)}, u32[]{:S(2)}) collective-permute-start(f32[2,8,16,1,128]{4,1,3,2,0:T(8,128)S(1)} %get-tuple-element.19), channel_id=1, source_target_pairs={{4,0},{8,4},{12,8},{16,12},{20,16},{24,20},{28,24},{5,1},{9,5},{13... | collective-permute-start | bytes 393224 | tf_op jit(solution)/shard_map/ppermute | solution.py:19
  81.7 8.9 %collective-permute-start.5 = (f32[2,8,1,34,128]{4,1,3,2,0:T(8,128)S(1)}, f32[2,8,1,34,128]{4,1,3,2,0:T(8,128)S(1)}, u32[]{:S(2)}, u32[]{:S(2)}) collective-permute-start(f32[2,8,1,34,128]{4,1,3,2,0:T(8,128)S(1)} %get-tuple-element.9), channel_id=1, source_target_pairs={{1,0},{2,1},{3,2},{5,4},{6,5},{7,6},{9,8},{10,9},{11,10},{13,12},{... | collective-permute-start | bytes 835592 | tf_op jit(solution)/shard_map/ppermute | solution.py:19
  83.0 9.3 %collective-permute-start.6 = (f32[2,8,1,34,128]{4,1,3,2,0:T(8,128)S(1)}, f32[2,8,1,34,128]{4,1,3,2,0:T(8,128)S(1)}, u32[]{:S(2)}, u32[]{:S(2)}) collective-permute-start(f32[2,8,1,34,128]{4,1,3,2,0:T(8,128)S(1)} %get-tuple-element.10), channel_id=1, source_target_pairs={{0,1},{1,2},{2,3},{4,5},{5,6},{6,7},{8,9},{9,10},{10,11},{12,13},{... | collective-permute-start | bytes 835592 | tf_op jit(solution)/shard_map/ppermute | solution.py:16
  97.0 5.6 %collective-permute-start.7 = (f32[2,8,16,1,128]{4,1,3,2,0:T(8,128)S(1)}, f32[2,8,16,1,128]{4,1,3,2,0:T(8,128)S(1)}, u32[]{:S(2)}, u32[]{:S(2)}) collective-permute-start(f32[2,8,16,1,128]{4,1,3,2,0:T(8,128)S(1)} %get-tuple-element.18), channel_id=1, source_target_pairs={{0,4},{4,8},{8,12},{12,16},{16,20},{20,24},{24,28},{1,5},{5,9},{9,... | collective-permute-start | bytes 393224 | tf_op jit(solution)/shard_map/ppermute | solution.py:16
  101.4 4.6 %collective-permute-start.8 = (f32[2,8,16,1,128]{4,1,3,2,0:T(8,128)S(1)}, f32[2,8,16,1,128]{4,1,3,2,0:T(8,128)S(1)}, u32[]{:S(2)}, u32[]{:S(2)}) collective-permute-start(f32[2,8,16,1,128]{4,1,3,2,0:T(8,128)S(1)} %get-tuple-element.17), channel_id=1, source_target_pairs={{4,0},{8,4},{12,8},{16,12},{20,16},{24,20},{28,24},{5,1},{9,5},{13... | collective-permute-start | bytes 393224 | tf_op jit(solution)/shard_map/ppermute | solution.py:19
  106.0 8.9 %collective-permute-start.10 = (f32[2,8,1,34,128]{4,1,3,2,0:T(8,128)S(1)}, f32[2,8,1,34,128]{4,1,3,2,0:T(8,128)S(1)}, u32[]{:S(2)}, u32[]{:S(2)}) collective-permute-start(f32[2,8,1,34,128]{4,1,3,2,0:T(8,128)S(1)} %get-tuple-element.8), channel_id=1, source_target_pairs={{0,1},{1,2},{2,3},{4,5},{5,6},{6,7},{8,9},{9,10},{10,11},{12,13},{... | collective-permute-start | bytes 835592 | tf_op jit(solution)/shard_map/ppermute | solution.py:16
  110.5 9.1 %collective-permute-start.9 = (f32[2,8,1,34,128]{4,1,3,2,0:T(8,128)S(1)}, f32[2,8,1,34,128]{4,1,3,2,0:T(8,128)S(1)}, u32[]{:S(2)}, u32[]{:S(2)}) collective-permute-start(f32[2,8,1,34,128]{4,1,3,2,0:T(8,128)S(1)} %get-tuple-element.7), channel_id=1, source_target_pairs={{1,0},{2,1},{3,2},{5,4},{6,5},{7,6},{9,8},{10,9},{11,10},{13,12},{... | collective-permute-start | bytes 835592 | tf_op jit(solution)/shard_map/ppermute | solution.py:19
where the time goes:
time: 166 us; the launch traced here: 165 us
  waiting for transfers between devices  44.7 us (27%)
  starting transfers between devices  43.6 us (26%)
  blocking collectives  32.7 us (20%)
  matrix products  23 us (14%)
  local copies, waits for them, and re-layouts  10.7 us (6%)
  other arithmetic  9.89 us (6%)
    all_to_all x1, blocking collectives, on_device(): lax.all_to_all(times.reshape(gathered.shape), 'tm', split_axis=0, concat_...  32.7 us
    all_to_all x1, waiting for transfers between devices, on_device(): lax.all_to_all(scaled, 'tm', split_axis=2, concat_axis=0, tiled=True)  26.4 us
    ppermute x5, starting transfers between devices, extended(): lax.ppermute(lax.slice_in_dim(block, block.shape[dim] - width, None, axis...  19.5 us
    ppermute x5, waiting for transfers between devices, extended(): lax.ppermute(lax.slice_in_dim(block, 0, width, axis=dim), axis, backward)  13.7 us
    all_to_all x1, starting transfers between devices, on_device(): lax.all_to_all(scaled, 'tm', split_axis=2, concat_axis=0, tiled=True)  13.5 us
    add x2, other arithmetic, relax(): field = divide(source + kappa_b * rims(field))  7.25 us
    ppermute x5, starting transfers between devices, extended(): lax.ppermute(lax.slice_in_dim(block, 0, width, axis=dim), axis, backward)  6.68 us
    dot_general x1, matrix products, on_device(): jnp.dot(residual.reshape(-1, column_size), basis, precision=highest)  4.88 us
  transfers between devices with their start and end apart: 12, of which 7 were waited for; matrix products, arithmetic and copies ran while one was open for 5% of the time, Pallas kernels for 0%

commit v1 on v0

--- a/solution.py
+++ b/solution.py
@@ -83,7 +83,10 @@
     )
     decay = jnp.log(ALPHA) / steps_total
     scaled = modal * jnp.exp(decay * here.astype(jnp.float32))
-    gathered = lax.all_to_all(scaled, "tm", split_axis=2, concat_axis=0, tiled=True)
+    gathered = jnp.concatenate(
+        lax.all_to_all(jnp.stack(jnp.split(scaled, lax.axis_size("tm"), axis=2)), "tm", 0, 0),
+        axis=0,
+    )
     block_y = gathered.shape[2]
     indices = jnp.arange(steps_total)
     steps_f = indices.astype(jnp.float32)

time: 166 us -> 167 us (level)
  matrix products: 23 us -> 24.9 us
    unnamed x12 -> x19, local copies, waits for them, and re-layouts: 2 us -> 7.07 us
    mul x1 -> x0, local copies, waits for them, and re-layouts: 2.54 us -> none  [on_device(): scaled = modal * jnp.exp(decay * here.astype(jnp.float32))]
    reshape x1 -> x0, local copies, waits for them, and re-layouts: 1.97 us -> none  [on_device(): flat_cells = gathered.reshape(steps_total, -1)]
    all_to_all x1 -> x0, local copies, waits for them, and re-layouts: 1.95 us -> none  [on_device(): lax.all_to_all(scaled, 'tm', split_axis=2, concat_axis=0, tiled=True)]
where the time goes in v1:
time: 167 us; the launch traced here: 166 us
  waiting for transfers between devices  44.7 us (27%)
  starting transfers between devices  43.6 us (26%)
  blocking collectives  32.7 us (20%)
  matrix products  24.9 us (15%)
  local copies, waits for them, and re-layouts  10 us (6%)
  other arithmetic  9.89 us (6%)
    all_to_all x1, blocking collectives, on_device(): lax.all_to_all(times.reshape(gathered.shape), 'tm', split_axis=0, concat_...  32.7 us
    all_to_all x1, waiting for transfers between devices, on_device(): lax.all_to_all(jnp.stack(jnp.split(scaled, lax.axis_size('tm'), axis=2)),...  26.4 us
    ppermute x5, starting transfers between devices, extended(): lax.ppermute(lax.slice_in_dim(block, block.shape[dim] - width, None, axis...  19.5 us
    ppermute x5, waiting for transfers between devices, extended(): lax.ppermute(lax.slice_in_dim(block, 0, width, axis=dim), axis, backward)  13.7 us
    all_to_all x1, starting transfers between devices, on_device(): lax.all_to_all(jnp.stack(jnp.split(scaled, lax.axis_size('tm'), axis=2)),...  13.5 us
    add x2, other arithmetic, relax(): field = divide(source + kappa_b * rims(field))  7.25 us
    unnamed x19, local copies, waits for them, and re-layouts  7.07 us
    ppermute x5, starting transfers between devices, extended(): lax.ppermute(lax.slice_in_dim(block, 0, width, axis=dim), axis, backward)  6.68 us
  transfers between devices with their start and end apart: 12, of which 7 were waited for; matrix products, arithmetic and copies ran while one was open for 5% of the time, Pallas kernels for 0%

profile of v1, /device:TPU:0, one launch (start us, length us, event | category | flops | bytes accessed | tf_op | source)
XLA Modules:
  0.0 166.2 jit_solution(3277758221123391601)
XLA Ops:
  0.0 3.9 %collective-permute-start = (f32[1,16,256,128]{3,2,1,0:T(8,128)}, f32[1,16,256,128]{3,2,1,0:T(8,128)}, u32[]{:S(2)}, u32[]{:S(2)}) collective-permute-start(f32[1,16,256,128]{3,2,1,0:T(8,128)} %param.6), channel_id=1, source_target_pairs={{0,4},{4,8},{8,12},{12,16},{16,20},{20,24},{24,28},{1,5},{5,9},{9,... | collective-permute-start | bytes 6291464 | tf_op jit(solution)/shard_map/ppermute | solution.py:27
  6.2 4.9 %collective-permute-start.2 = (f32[1,1,256,128]{3,2,1,0:T(8,128)S(1)}, f32[1,1,256,128]{3,2,1,0:T(8,128)S(1)}, u32[]{:S(2)}, u32[]{:S(2)}) collective-permute-start(f32[1,1,256,128]{3,2,1,0:T(8,128)S(1)} %get-tuple-element.21), channel_id=1, source_target_pairs={{0,1},{1,2},{2,3},{4,5},{5,6},{6,7},{8,9},{9,10},{10,11},{12,13},{... | collective-permute-start | bytes 393224 | tf_op jit(solution)/shard_map/ppermute | solution.py:16
  11.1 3.4 %convolution_multiply_fusion = f32[4096,128]{1,0:T(8,128)S(1)} fusion(f32[4096,128]{1,0:T(8,128)} %bitcast.92, f32[128,128]{1,0:T(8,128)S(1)} %copy-done, f32[128]{0:T(128)} %param.10), kind=kOutput, calls=%fused_computation.8 | convolution fusion | flops 805830656 | bytes 4260352 | tf_op jit(solution)/shard_map/dot_general | solution.py:71
  14.6 3.1 %fusion.108 = f32[4096,128]{1,0:T(8,128)} fusion(f32[4096,128]{1,0:T(8,128)S(1)} %convolution_multiply_fusion, f32[128,128]{1,0:T(8,128)S(1)} %copy-done), kind=kOutput, calls=%fused_computation.178 | convolution fusion | flops 805306368 | bytes 4259840 | tf_op jit(solution)/shard_map/dot_general | solution.py:72
  20.0 4.9 %multiply_bitcast_fusion = f32[1,16,256,128]{3,2,1,0:T(8,128)S(1)} fusion(f32[1,16,256,128]{3,2,1,0:T(8,128)S(1)} %copy-done.1, f32[1,18,258,128]{3,2,1,0:T(8,128)S(1)} %select_maximum_fusion, f32[1,1,256,128]{3,2,1,0:T(8,128)S(1)} %collective-permute-done.2, f32[1,1,256,128]{3,2,1,0:T(8,128)S(1)} %collective-permute-done.1, ...), kind=kOutput, calls=%fused_computation.89 | convolution fusion | flops 815792128 | bytes 17121284 | tf_op jit(solution)/shard_map/dot_general | solution.py:81
  30.7 13.5 %all-to-all-start = ((f32[8,1,16,32,128]{4,3,2,1,0:T(8,128)}), f32[8,1,16,32,128]{4,3,2,1,0:T(8,128)S(1)}, u32[]{:S(2)}, u32[]{:S(2)}) async-start(f32[8,1,16,32,128]{4,3,2,1,0:T(8,128)} %fusion.63), calls=%async_computation | async-start | bytes 4194304 | tf_op jit(solution)/shard_map/all_to_all | solution.py:87
  44.4 26.4 %all-to-all-done = f32[8,1,16,32,128]{4,3,2,1,0:T(8,128)S(1)} async-done(((f32[8,1,16,32,128]{4,3,2,1,0:T(8,128)}), f32[8,1,16,32,128]{4,3,2,1,0:T(8,128)S(1)}, u32[]{:S(2)}, u32[]{:S(2)}) %all-to-all-start) | async-done | bytes 2097184 | tf_op jit(solution)/shard_map/all_to_all | solution.py:87
  70.8 2.9 %fusion.26 = f32[8,65536]{1,0:T(8,128)S(1)} fusion(f32[1,8,512,128]{3,2,1,0:T(8,128)S(1)} %bitcast.90), kind=kOutput, calls=%fused_computation.65 | convolution fusion | flops 50332544 | bytes 4194304 | tf_op jit(solution)/shard_map/dot_general | solution.py:100
  73.7 2.9 %convolution_negate_fusion = f32[8,65536]{1,0:T(8,128)S(1)} fusion(f32[1,8,512,128]{3,2,1,0:T(8,128)S(1)} %bitcast.91), kind=kOutput, calls=%fused_computation.2 | convolution fusion | flops 50856832 | bytes 4194304 | tf_op jit(solution)/shard_map/dot_general | solution.py:101
  80.3 2.7 %collective-permute-done.4 = f32[2,8,16,1,128]{4,1,3,2,0:T(8,128)S(1)} collective-permute-done((f32[2,8,16,1,128]{4,1,3,2,0:T(8,128)S(1)}, f32[2,8,16,1,128]{4,1,3,2,0:T(8,128)S(1)}, u32[]{:S(2)}, u32[]{:S(2)}) %collective-permute-start.4) | collective-permute-done | bytes 131104 | tf_op jit(solution)/shard_map/ppermute | solution.py:19
  84.3 4.6 %collective-permute-start.6 = (f32[2,8,1,34,128]{4,1,3,2,0:T(8,128)S(1)}, f32[2,8,1,34,128]{4,1,3,2,0:T(8,128)S(1)}, u32[]{:S(2)}, u32[]{:S(2)}) collective-permute-start(f32[2,8,1,34,128]{4,1,3,2,0:T(8,128)S(1)} %get-tuple-element.10), channel_id=1, source_target_pairs={{0,1},{1,2},{2,3},{4,5},{5,6},{6,7},{8,9},{9,10},{10,11},{12,13},{... | collective-permute-start | bytes 835592 | tf_op jit(solution)/shard_map/ppermute | solution.py:16
  88.9 3.0 %collective-permute-done.5 = f32[2,8,1,34,128]{4,1,3,2,0:T(8,128)S(1)} collective-permute-done((f32[2,8,1,34,128]{4,1,3,2,0:T(8,128)S(1)}, f32[2,8,1,34,128]{4,1,3,2,0:T(8,128)S(1)}, u32[]{:S(2)}, u32[]{:S(2)}) %collective-permute-start.5) | collective-permute-done | bytes 278560 | tf_op jit(solution)/shard_map/ppermute | solution.py:19
  91.9 1.7 %collective-permute-done.6 = f32[2,8,1,34,128]{4,1,3,2,0:T(8,128)S(1)} collective-permute-done((f32[2,8,1,34,128]{4,1,3,2,0:T(8,128)S(1)}, f32[2,8,1,34,128]{4,1,3,2,0:T(8,128)S(1)}, u32[]{:S(2)}, u32[]{:S(2)}) %collective-permute-start.6) | collective-permute-done | bytes 278560 | tf_op jit(solution)/shard_map/ppermute | solution.py:16
  93.6 3.6 %fusion.8 = f32[2,8,16,32,128]{4,1,3,2,0:T(8,128)S(1)} fusion(f32[2,8,16,1,128]{4,1,3,2,0:T(8,128)S(1)} %collective-permute-done.3, f32[1,8,16,32,128]{4,1,3,2,0:T(8,128)S(1)} %get-tuple-element.14, f32[1,8,16,32,128]{4,1,3,2,0:T(8,128)S(1)} %get-tuple-element.13, f32[2,8,16,1,128]{4,1,3,2,0:T(8,128)S(1)} %collective-permute-done.4, ...), kind=kLoop, calls=%fused_computation.29 | loop fusion | flops 18874368 | bytes 13404160 | tf_op jit(solution)/shard_map/add | solution.py:52
  98.3 4.3 %collective-permute-start.7 = (f32[2,8,16,1,128]{4,1,3,2,0:T(8,128)S(1)}, f32[2,8,16,1,128]{4,1,3,2,0:T(8,128)S(1)}, u32[]{:S(2)}, u32[]{:S(2)}) collective-permute-start(f32[2,8,16,1,128]{4,1,3,2,0:T(8,128)S(1)} %get-tuple-element.18), channel_id=1, source_target_pairs={{0,4},{4,8},{8,12},{12,16},{16,20},{20,24},{24,28},{1,5},{5,9},{9,... | collective-permute-start | bytes 393224 | tf_op jit(solution)/shard_map/ppermute | solution.py:16
  104.0 3.3 %collective-permute-done.8 = f32[2,8,16,1,128]{4,1,3,2,0:T(8,128)S(1)} collective-permute-done((f32[2,8,16,1,128]{4,1,3,2,0:T(8,128)S(1)}, f32[2,8,16,1,128]{4,1,3,2,0:T(8,128)S(1)}, u32[]{:S(2)}, u32[]{:S(2)}) %collective-permute-start.8) | collective-permute-done | bytes 131104 | tf_op jit(solution)/shard_map/ppermute | solution.py:19
  107.3 4.4 %collective-permute-start.10 = (f32[2,8,1,34,128]{4,1,3,2,0:T(8,128)S(1)}, f32[2,8,1,34,128]{4,1,3,2,0:T(8,128)S(1)}, u32[]{:S(2)}, u32[]{:S(2)}) collective-permute-start(f32[2,8,1,34,128]{4,1,3,2,0:T(8,128)S(1)} %get-tuple-element.8), channel_id=1, source_target_pairs={{0,1},{1,2},{2,3},{4,5},{5,6},{6,7},{8,9},{9,10},{10,11},{12,13},{... | collective-permute-start | bytes 835592 | tf_op jit(solution)/shard_map/ppermute | solution.py:16
  113.3 2.9 %collective-permute-done.10 = f32[2,8,1,34,128]{4,1,3,2,0:T(8,128)S(1)} collective-permute-done((f32[2,8,1,34,128]{4,1,3,2,0:T(8,128)S(1)}, f32[2,8,1,34,128]{4,1,3,2,0:T(8,128)S(1)}, u32[]{:S(2)}, u32[]{:S(2)}) %collective-permute-start.10) | collective-permute-done | bytes 278560 | tf_op jit(solution)/shard_map/ppermute | solution.py:16
  116.2 4.7 %collective-permute-done.9 = f32[2,8,1,34,128]{4,1,3,2,0:T(8,128)S(1)} collective-permute-done((f32[2,8,1,34,128]{4,1,3,2,0:T(8,128)S(1)}, f32[2,8,1,34,128]{4,1,3,2,0:T(8,128)S(1)}, u32[]{:S(2)}, u32[]{:S(2)}) %collective-permute-start.9) | collective-permute-done | bytes 278560 | tf_op jit(solution)/shard_map/ppermute | solution.py:19
  120.9 3.6 %fusion.3 = f32[2,8,16,32,128]{4,1,3,2,0:T(8,128)S(1)} fusion(f32[2,8,16,1,128]{4,1,3,2,0:T(8,128)S(1)} %collective-permute-done.7, f32[1,8,16,32,128]{4,1,3,2,0:T(8,128)S(1)} %get-tuple-element.12, f32[1,8,16,32,128]{4,1,3,2,0:T(8,128)S(1)} %get-tuple-element.11, f32[2,8,16,1,128]{4,1,3,2,0:T(8,128)S(1)} %collective-permute-done.8, ...), kind=kLoop, calls=%fused_computation.12 | loop fusion | flops 18874368 | bytes 13404160 | tf_op jit(solution)/shard_map/add | solution.py:52
  125.1 2.2 %fusion.39 = f32[8,65536]{1,0:T(8,128)S(1)} fusion(f32[8,65536]{1,0:T(8,128)S(1)} %bitcast.101, f32[8,65536]{1,0:T(8,128)S(1)} %bitcast.99, f32[8,65536]{1,0:T(8,128)S(1)} %bitcast.96, f32[8]{0:T(128)S(1)} %get-tuple-element.24, f32[8]{0:T(128)S(1)} %get-tuple-element.23, f32[65536]{0:T(1024)S(1)} %bitcast.103), kind=kOutput, calls=%fused_computation.83 | convolution fusion | flops 54002560 | bytes 8650816 | tf_op jit(solution)/shard_map/dot_general | solution.py:116
  127.4 2.4 %fusion = f32[8,65536]{1,0:T(8,128)S(1)} fusion(f32[8,65536]{1,0:T(8,128)S(1)} %fusion.39, f32[8,65536]{1,0:T(8,128)S(1)} %bitcast.100, f32[8,65536]{1,0:T(8,128)S(1)} %bitcast.102, f32[8,65536]{1,0:T(8,128)S(1)} %bitcast.97, f32[8]{0:T(128)S(1)} %exponential_multiply_fusion, f32[8]{0:T(128)S(1)} %get-tuple-element.24, f32[8]{0:T(128)S(1)} %get-tuple-element.23, ...), kind=kOutput, calls=%fused_computation.1 | convolution fusion | flops 55051136 | bytes 10748000 | tf_op jit(solution)/shard_map/dot_general | solution.py:116
  130.2 32.7 %all_to_all.20 = f32[8,16,32,128]{3,2,1,0:T(8,128)S(1)} all-to-all(f32[8,16,32,128]{3,2,1,0:T(8,128)S(1)} %copy.8), channel_id=1, replica_groups=mesh['tm'=8,'tx'=4] {'tm'}, dimensions={0} | all-to-all | bytes 4194304 | tf_op jit(solution)/shard_map/all_to_all | solution.py:119
  163.1 3.1 %convolution_bitcast_fusion = f32[1,16,256,128]{3,2,1,0:T(8,128)} fusion(f32[16,256,128]{2,1,0:T(8,128)S(1)} %bitcast.94, f32[128,128]{1,0:T(8,128)S(1)} %copy-done), kind=kOutput, calls=%fused_computation.95 | convolution fusion | flops 805306368 | bytes 4259840 | tf_op jit(solution)/shard_map/dot_general | solution.py:122
  (49 shorter events, 20.7 us)
Async XLA Ops:
  0.0 11.1 %copy-start = (f32[128,128]{1,0:T(8,128)S(1)}, f32[128,128]{1,0:T(8,128)}, u32[]{:S(2)}) copy-start(f32[128,128]{1,0:T(8,128)} %param.11) | copy-start | bytes 196612
  0.0 18.0 %collective-permute-start = (f32[1,16,256,128]{3,2,1,0:T(8,128)}, f32[1,16,256,128]{3,2,1,0:T(8,128)}, u32[]{:S(2)}, u32[]{:S(2)}) collective-permute-start(f32[1,16,256,128]{3,2,1,0:T(8,128)} %param.6), channel_id=1, source_target_pairs={{0,4},{4,8},{8,12},{12,16},{16,20},{20,24},{24,28},{1,5},{5,9},{9,... | collective-permute-start | bytes 6291464 | tf_op jit(solution)/shard_map/ppermute | solution.py:27
  4.9 12.9 %collective-permute-start.1 = (f32[1,1,256,128]{3,2,1,0:T(8,128)S(1)}, f32[1,1,256,128]{3,2,1,0:T(8,128)S(1)}, u32[]{:S(2)}, u32[]{:S(2)}) collective-permute-start(f32[1,1,256,128]{3,2,1,0:T(8,128)S(1)} %get-tuple-element.22), channel_id=1, source_target_pairs={{1,0},{2,1},{3,2},{5,4},{6,5},{7,6},{9,8},{10,9},{11,10},{13,12},{... | collective-permute-start | bytes 393224 | tf_op jit(solution)/shard_map/ppermute | solution.py:19
  6.2 11.6 %collective-permute-start.2 = (f32[1,1,256,128]{3,2,1,0:T(8,128)S(1)}, f32[1,1,256,128]{3,2,1,0:T(8,128)S(1)}, u32[]{:S(2)}, u32[]{:S(2)}) collective-permute-start(f32[1,1,256,128]{3,2,1,0:T(8,128)S(1)} %get-tuple-element.21), channel_id=1, source_target_pairs={{0,1},{1,2},{2,3},{4,5},{5,6},{6,7},{8,9},{9,10},{10,11},{12,13},{... | collective-permute-start | bytes 393224 | tf_op jit(solution)/shard_map/ppermute | solution.py:16
  14.6 3.2 %copy-start.1 = (f32[1,16,256,128]{3,2,1,0:T(8,128)S(1)}, f32[1,16,256,128]{3,2,1,0:T(8,128)}, u32[]{:S(2)}) copy-start(f32[1,16,256,128]{3,2,1,0:T(8,128)} %param.6) | copy-start | bytes 6291460
  17.7 1.6 copy-start.2
  17.7 1.6 copy-start.3
  17.8 2.2 %copy-start.5 = (f32[1,16,256,128]{3,2,1,0:T(8,128)S(1)}, f32[1,16,256,128]{3,2,1,0:T(8,128)}, u32[]{:S(2)}) copy-start(f32[1,16,256,128]{3,2,1,0:T(8,128)} %param.7) | copy-start | bytes 6291460
  30.7 13.7 %copy-start.4 = (f32[128]{0:T(128)S(1)}, f32[128]{0:T(128)}, u32[]{:S(2)}) copy-start(f32[128]{0:T(128)} %param.10) | copy-start | bytes 1540
  30.7 40.1 %all-to-all-start = ((f32[8,1,16,32,128]{4,3,2,1,0:T(8,128)}), f32[8,1,16,32,128]{4,3,2,1,0:T(8,128)S(1)}, u32[]{:S(2)}, u32[]{:S(2)}) async-start(f32[8,1,16,32,128]{4,3,2,1,0:T(8,128)} %fusion.63), calls=%async_computation | async-start | bytes 4194304 | tf_op jit(solution)/shard_map/all_to_all | solution.py:87
  77.7 2.6 %collective-permute-start.3 = (f32[2,8,16,1,128]{4,1,3,2,0:T(8,128)S(1)}, f32[2,8,16,1,128]{4,1,3,2,0:T(8,128)S(1)}, u32[]{:S(2)}, u32[]{:S(2)}) collective-permute-start(f32[2,8,16,1,128]{4,1,3,2,0:T(8,128)S(1)} %get-tuple-element.20), channel_id=1, source_target_pairs={{0,4},{4,8},{8,12},{12,16},{16,20},{20,24},{24,28},{1,5},{5,9},{9,... | collective-permute-start | bytes 393224 | tf_op jit(solution)/shard_map/ppermute | solution.py:16
  79.0 4.0 %collective-permute-start.4 = (f32[2,8,16,1,128]{4,1,3,2,0:T(8,128)S(1)}, f32[2,8,16,1,128]{4,1,3,2,0:T(8,128)S(1)}, u32[]{:S(2)}, u32[]{:S(2)}) collective-permute-start(f32[2,8,16,1,128]{4,1,3,2,0:T(8,128)S(1)} %get-tuple-element.19), channel_id=1, source_target_pairs={{4,0},{8,4},{12,8},{16,12},{20,16},{24,20},{28,24},{5,1},{9,5},{13... | collective-permute-start | bytes 393224 | tf_op jit(solution)/shard_map/ppermute | solution.py:19
  83.0 8.9 %collective-permute-start.5 = (f32[2,8,1,34,128]{4,1,3,2,0:T(8,128)S(1)}, f32[2,8,1,34,128]{4,1,3,2,0:T(8,128)S(1)}, u32[]{:S(2)}, u32[]{:S(2)}) collective-permute-start(f32[2,8,1,34,128]{4,1,3,2,0:T(8,128)S(1)} %get-tuple-element.9), channel_id=1, source_target_pairs={{1,0},{2,1},{3,2},{5,4},{6,5},{7,6},{9,8},{10,9},{11,10},{13,12},{... | collective-permute-start | bytes 835592 | tf_op jit(solution)/shard_map/ppermute | solution.py:19
  84.3 9.3 %collective-permute-start.6 = (f32[2,8,1,34,128]{4,1,3,2,0:T(8,128)S(1)}, f32[2,8,1,34,128]{4,1,3,2,0:T(8,128)S(1)}, u32[]{:S(2)}, u32[]{:S(2)}) collective-permute-start(f32[2,8,1,34,128]{4,1,3,2,0:T(8,128)S(1)} %get-tuple-element.10), channel_id=1, source_target_pairs={{0,1},{1,2},{2,3},{4,5},{5,6},{6,7},{8,9},{9,10},{10,11},{12,13},{... | collective-permute-start | bytes 835592 | tf_op jit(solution)/shard_map/ppermute | solution.py:16
  98.3 5.6 %collective-permute-start.7 = (f32[2,8,16,1,128]{4,1,3,2,0:T(8,128)S(1)}, f32[2,8,16,1,128]{4,1,3,2,0:T(8,128)S(1)}, u32[]{:S(2)}, u32[]{:S(2)}) collective-permute-start(f32[2,8,16,1,128]{4,1,3,2,0:T(8,128)S(1)} %get-tuple-element.18), channel_id=1, source_target_pairs={{0,4},{4,8},{8,12},{12,16},{16,20},{20,24},{24,28},{1,5},{5,9},{9,... | collective-permute-start | bytes 393224 | tf_op jit(solution)/shard_map/ppermute | solution.py:16
  102.7 4.6 %collective-permute-start.8 = (f32[2,8,16,1,128]{4,1,3,2,0:T(8,128)S(1)}, f32[2,8,16,1,128]{4,1,3,2,0:T(8,128)S(1)}, u32[]{:S(2)}, u32[]{:S(2)}) collective-permute-start(f32[2,8,16,1,128]{4,1,3,2,0:T(8,128)S(1)} %get-tuple-element.17), channel_id=1, source_target_pairs={{4,0},{8,4},{12,8},{16,12},{20,16},{24,20},{28,24},{5,1},{9,5},{13... | collective-permute-start | bytes 393224 | tf_op jit(solution)/shard_map/ppermute | solution.py:19
  107.3 8.9 %collective-permute-start.10 = (f32[2,8,1,34,128]{4,1,3,2,0:T(8,128)S(1)}, f32[2,8,1,34,128]{4,1,3,2,0:T(8,128)S(1)}, u32[]{:S(2)}, u32[]{:S(2)}) collective-permute-start(f32[2,8,1,34,128]{4,1,3,2,0:T(8,128)S(1)} %get-tuple-element.8), channel_id=1, source_target_pairs={{0,1},{1,2},{2,3},{4,5},{5,6},{6,7},{8,9},{9,10},{10,11},{12,13},{... | collective-permute-start | bytes 835592 | tf_op jit(solution)/shard_map/ppermute | solution.py:16
  111.8 9.1 %collective-permute-start.9 = (f32[2,8,1,34,128]{4,1,3,2,0:T(8,128)S(1)}, f32[2,8,1,34,128]{4,1,3,2,0:T(8,128)S(1)}, u32[]{:S(2)}, u32[]{:S(2)}) collective-permute-start(f32[2,8,1,34,128]{4,1,3,2,0:T(8,128)S(1)} %get-tuple-element.7), channel_id=1, source_target_pairs={{1,0},{2,1},{3,2},{5,4},{6,5},{7,6},{9,8},{10,9},{11,10},{13,12},{... | collective-permute-start | bytes 835592 | tf_op jit(solution)/shard_map/ppermute | solution.py:19
